TPU v7x, 128 devices: a whole 4x4x4 slice. The times are simulated.
128 devices in a mesh: dp: 8 (over x_lo, y), expert: 16 (over z, x_hi, core).
Axes of the slice: x: 4 (x_hi: 2, x_lo: 2; x = x_hi * 2 + x_lo), y: 4, z: 4, core: 2. Of those that a mesh axis runs over, the one named last changes fastest.
Arguments:
- tokens: bfloat16 [16384, 1536], P(('dp', 'expert')), may hold values from -6 to 6
- gate_prob: float32 [16384], P(('dp', 'expert')), may hold values from 0.2 to 1
- expert_index: int32 [16384], P(('dp', 'expert')), may hold values from 0 to 31, as said below
- slot_index: int32 [16384], P(('dp', 'expert')), may hold values from 0 to 127, as said below
- dropped: int32 [16384], P(('dp', 'expert')), may hold values from 0 to 1
- cotangent: bfloat16 [16384, 1536], P(('dp', 'expert')), may hold values from -6 to 6
- expert_in: bfloat16 [32, 1536, 6144], P('expert', None, 'dp'), may hold values from -0.15625 to 0.15625
- expert_out: bfloat16 [32, 6144, 1536], P('expert', 'dp'), may hold values from -0.078125 to 0.078125
- residual_in: bfloat16 [1536, 3072], P(None, 'dp'), may hold values from -0.15625 to 0.15625
- residual_out: bfloat16 [3072, 1536], P('dp'), may hold values from -0.109375 to 0.109375
Outputs:
- output: bfloat16 [16384, 1536], P(('dp', 'expert'))
- grad_tokens: bfloat16 [16384, 1536], P(('dp', 'expert'))
- grad_gate: float32 [16384], P(('dp', 'expert'))
- grad_expert_in: bfloat16 [32, 1536, 6144], P('expert', None, 'dp')
- grad_expert_out: bfloat16 [32, 6144, 1536], P('expert', 'dp')
- grad_residual_in: bfloat16 [1536, 3072], P(None, 'dp')
- grad_residual_out: bfloat16 [3072, 1536], P('dp')
Inputs may be any that keep to these rules, and one draw needn't show every extreme that they name: `expert_index`: on every device, at least 7 tokens choose one expert, the same expert on all devices, and the tokens in its first 5 slots are not dropped. `slot_index`: on each device the tokens of one expert hold the slots 0 to n - 1 once each, n being their count; dropped tokens take the highest slots of their expert; on some device all tokens choose one expert.
All inputs are finite; a program needn't handle non-finite values.
Results may differ from a plain program's by a relative error of at most 0.018.
Values may be sent and summed in bfloat16 or wider, within the bound.
No kernel may reach another device: no remote copies, remote signals or barrier semaphores. Data moves between devices by JAX's collectives and lax.ppermute only.
A program may use at most 192 MiB of HBM per device.

v0:
```python
import jax
import jax.numpy as jnp
from jax import lax
from jax.sharding import Mesh
from jax.sharding import PartitionSpec as P

EXPERT = ("expert_0", "expert_1", "expert_2")
DP_EXPERT = ("dp", "expert_0", "expert_1", "expert_2")


def in_blocks(value, dim, peers):
    before, after = (value.shape[:dim], value.shape[dim + 1 :])
    return jnp.moveaxis(value.reshape(*before, peers, -1, *after), dim, 0)


def in_order(blocks, dim):
    lengths = list(blocks.shape[1:])
    lengths[dim] *= blocks.shape[0]
    return jnp.moveaxis(blocks, 0, dim).reshape(lengths)


def exchange_in_order(blocks, axes, turns):
    inside = blocks.shape[1:]
    whole = blocks.reshape(*(lax.axis_size(a) for a in axes), *inside)
    for k in turns:
        whole = lax.all_to_all(whole, axes[k], k, k, tiled=True)
    return whole.reshape(-1, *inside)


def exchange_by_chip(value, groups, turns, split_dim, concat_dim):
    peers = lax.axis_size(groups[0]) * lax.axis_size(groups[1])
    blocks = in_blocks(value, split_dim, peers)
    return in_order(exchange_in_order(blocks, groups, turns), concat_dim)


def sum_packed(arrays, axis, dims):
    peers = lax.axis_size(axis)
    blocks = [in_blocks(a, dim, peers) for a, dim in zip(arrays, dims)]
    lines = jnp.concatenate([b.reshape(peers, -1) for b in blocks], axis=1)
    rows = max(16, -(-lines.shape[1] // 1024) * 8)
    lines = jnp.pad(lines, ((0, 0), (0, rows * 128 - lines.shape[1]))).reshape(-1, 128)
    flat, at, gathered = (lax.psum_scatter(lines, axis, tiled=True).reshape(-1), 0, [])
    for b in blocks:
        part = b[0]
        gathered.append(flat[at : at + part.size].reshape(part.shape))
        at += part.size
    return tuple(gathered)


def in_one(arrays, axis):
    flat, at, gathered = (jnp.concatenate([a.reshape(-1) for a in arrays]), 0, [])
    running = lax.psum(flat, axis)
    for a in arrays:
        gathered.append(running[at : at + a.size].reshape(a.shape))
        at += a.size
    return tuple(gathered)


def gelu_tanh(values):
    return jax.nn.gelu(values, approximate=True)


def place_rows(values, position, slot_count):
    buffer = jnp.zeros((slot_count + 1, values.shape[1]), values.dtype)
    return buffer.at[position].set(values)[:slot_count]


def fetch_rows(buffer, position):
    padded = jnp.concatenate([buffer, jnp.zeros((1, buffer.shape[1]), buffer.dtype)], axis=0)
    return padded[position]


def on_device(
    tokens,
    gate_prob,
    expert_index,
    slot_index,
    dropped,
    cotangent,
    expert_in,
    expert_out,
    residual_in,
    residual_out,
):
    groups = lax.axis_size("dp")
    host_count = lax.axis_size(EXPERT)
    local_count = expert_in.shape[0]
    experts_all = local_count * host_count
    row_count, model_width = tokens.shape
    capacity = max(2, 5 * row_count // (4 * experts_all))
    kept = (dropped == 0) & (slot_index < capacity)
    kept_float = kept.astype(jnp.float32)
    gate_kept = gate_prob * kept_float
    own_slots = experts_all * capacity
    own_index = jnp.where(kept, expert_index * capacity + slot_index, -1)
    own_position = jnp.where(kept, own_index, own_slots)

    def to_column(row_values, row_scale):
        values = (row_values.astype(jnp.float32) * row_scale[:, None]).astype(jnp.bfloat16)
        own_buffer = place_rows(values, own_position, own_slots).reshape(
            host_count, local_count, capacity, model_width
        )
        arrived = exchange_by_chip(own_buffer, (("expert_0", "expert_1"), "expert_2"), (1, 0), 0, 0)
        col_rows, column = (
            lax.all_gather(row_values, "dp", axis=0, tiled=True),
            lax.all_gather(arrived[None], "dp", axis=0, tiled=True),
        )
        return (col_rows, column)

    def from_column(dense_part, expert_part):
        dense_sum, expert_sum = tuple(
            (
                part.astype(jnp.float32)
                for part in sum_packed(
                    (dense_part.astype(jnp.bfloat16), expert_part.astype(jnp.bfloat16)),
                    "dp",
                    (0, 0),
                )
            )
        )
        own_result = lax.all_to_all(
            expert_sum[0].astype(jnp.bfloat16), EXPERT, split_axis=0, concat_axis=0, tiled=True
        )
        return (dense_sum[0], own_result.reshape(own_slots, model_width))

    unit_scale = jnp.ones_like(gate_prob)
    col_tokens, column = to_column(tokens, unit_scale)
    pre_expert = jnp.einsum(
        "abjcd,jdf->abjcf", column, expert_in, preferred_element_type=jnp.float32
    )
    hidden_f, expert_back = jax.vjp(gelu_tanh, pre_expert)
    hidden = hidden_f.astype(jnp.bfloat16)
    expert_part = jnp.einsum(
        "abjcf,jfd->abjcd", hidden, expert_out, preferred_element_type=jnp.float32
    )
    pre_dense = jnp.dot(col_tokens, residual_in, preferred_element_type=jnp.float32)
    dense_f, dense_back = jax.vjp(gelu_tanh, pre_dense)
    dense_hidden = dense_f.astype(jnp.bfloat16)
    dense_part = jnp.dot(dense_hidden, residual_out, preferred_element_type=jnp.float32).reshape(
        groups, row_count, model_width
    )
    dense_sum, expert_rows = from_column(dense_part, expert_part)
    expert_token = fetch_rows(expert_rows, own_position).astype(jnp.float32)
    output = (dense_sum + gate_kept[:, None] * expert_token).astype(jnp.bfloat16)
    grad_gate = kept_float * jnp.sum(cotangent.astype(jnp.float32) * expert_token, axis=1)
    col_cotangent, grad_column = to_column(cotangent, gate_kept)
    grad_hidden = jnp.einsum(
        "abjcd,jfd->abjcf", grad_column, expert_out, preferred_element_type=jnp.float32
    )
    grad_pre = expert_back(grad_hidden)[0].astype(jnp.bfloat16)
    grad_expert_out = jnp.einsum(
        "abjcf,abjcd->jfd", hidden, grad_column, preferred_element_type=jnp.float32
    ).astype(jnp.bfloat16)
    grad_expert_in = jnp.einsum(
        "abjcd,abjcf->jdf", column, grad_pre, preferred_element_type=jnp.float32
    ).astype(jnp.bfloat16)
    expert_dx = jnp.einsum(
        "abjcf,jdf->abjcd", grad_pre, expert_in, preferred_element_type=jnp.float32
    )
    dense_grad_hidden = jnp.einsum(
        "td,fd->tf", col_cotangent, residual_out, preferred_element_type=jnp.float32
    )
    dense_grad_pre = dense_back(dense_grad_hidden)[0].astype(jnp.bfloat16)
    out_partial = jnp.einsum(
        "tf,td->fd", dense_hidden, col_cotangent, preferred_element_type=jnp.float32
    )
    in_partial = jnp.einsum(
        "td,tf->df", col_tokens, dense_grad_pre, preferred_element_type=jnp.float32
    )
    in_total, out_total = tuple(
        (
            part.astype(jnp.float32)
            for part in in_one(
                (in_partial.astype(jnp.bfloat16), out_partial.astype(jnp.bfloat16)), EXPERT
            )
        )
    )
    dense_dx = jnp.einsum(
        "tf,df->td", dense_grad_pre, residual_in, preferred_element_type=jnp.float32
    ).reshape(groups, row_count, model_width)
    dense_dx_sum, expert_dx_rows = from_column(dense_dx, expert_dx)
    grad_tokens = (
        dense_dx_sum + fetch_rows(expert_dx_rows, own_position).astype(jnp.float32)
    ).astype(jnp.bfloat16)
    return (
        output,
        grad_tokens,
        grad_gate,
        grad_expert_in,
        grad_expert_out,
        in_total.astype(jnp.bfloat16),
        out_total.astype(jnp.bfloat16),
    )


def solution(mesh):
    finer = Mesh(
        mesh.devices.reshape(mesh.shape["dp"], 4, 2, 2), ("dp", "expert_0", "expert_1", "expert_2")
    )
    in_specs = (
        P(DP_EXPERT, None),
        P(DP_EXPERT),
        P(DP_EXPERT),
        P(DP_EXPERT),
        P(DP_EXPERT),
        P(DP_EXPERT, None),
        P(EXPERT, None, "dp"),
        P(EXPERT, "dp", None),
        P(None, "dp"),
        P("dp", None),
    )
    out_specs = (
        P(DP_EXPERT, None),
        P(DP_EXPERT, None),
        P(DP_EXPERT),
        P(EXPERT, None, "dp"),
        P(EXPERT, "dp", None),
        P(None, "dp"),
        P("dp", None),
    )
    return jax.shard_map(
        on_device, mesh=finer, in_specs=in_specs, out_specs=out_specs, check_vma=False
    )
```

profile of v0, /device:TPU:1, one launch (start us, length us, event | category | flops | bytes accessed | tf_op | source)
XLA Modules:
  0.0 565.7 jit_solution(12791289579129211362)
XLA Ops:
  9.4 1.8 scatter_custom_fusion
  11.8 5.1 all_to_all.30
  17.4 21.9 %all_to_all.31 = bf16[8,2,1,2,5,1536]{5,3,4,2,1,0:T(2,128)(2,1)S(1)} all-to-all(bf16[8,2,1,2,5,1536]{5,3,4,2,1,0:T(2,128)(2,1)S(1)} %copy.23), channel_id=1, replica_groups=mesh['dp'=8,'expert_0'=4,'expert_1'=2,'expert_2'=2] {'expert_0','expert_1'}, dimensions={0} | all-to-all | bytes 983040 | tf_op jit(solution)/shard_map/all_to_all | solution.py:26
  39.2 0.8 copy.43
  40.7 1.4 scatter_custom_fusion.1
  42.7 6.4 %all_to_all.32 = bf16[8,2,1,2,5,1536]{5,0,4,3,2,1:T(8,128)(2,1)S(1)} all-to-all(bf16[8,2,1,2,5,1536]{5,0,4,3,2,1:T(8,128)(2,1)S(1)} %copy.28), channel_id=1, replica_groups=mesh['dp'=8,'expert_0'=4,'expert_1'=2,'expert_2'=2] {'expert_2'}, dimensions={1} | all-to-all | bytes 983040 | tf_op jit(solution)/shard_map/all_to_all | solution.py:26
  49.1 1.2 copy.29
  50.2 3.5 all-to-all-start.4
  54.4 14.5 %all-to-all-done.4 = bf16[8,2,1,2,5,1536]{5,3,4,2,1,0:T(2,128)(2,1)S(1)} async-done(((bf16[8,2,1,2,5,1536]{5,3,4,2,1,0:T(2,128)(2,1)}), bf16[8,2,1,2,5,1536]{5,3,4,2,1,0:T(2,128)(2,1)S(1)}, u32[]{:S(2)}, u32[]{:S(2)}) %all-to-all-start.4) | async-done | bytes 491552 | tf_op jit(solution)/shard_map/all_to_all | solution.py:26
  68.9 0.9 copy.44
  70.1 4.8 fusion.56
  74.9 33.2 %all-gather.5.cloned.1.call-done = bf16[1024,1536]{1,0:T(8,128)(2,1)} async-done(((bf16[128,1536]{1,0:T(8,128)(2,1)}), bf16[1024,1536]{1,0:T(8,128)(2,1)}) %all-gather.5.cloned.1.call-update) | async-done | bytes 3145744 | tf_op jit(solution)/shard_map/all_gather | solution.py:105
  108.1 6.1 %fusion.44 = (bf16[1024,384]{1,0:T(8,128)(2,1)S(1)}, f32[1024,384]{1,0:T(8,128)}) fusion(f32[1024,384]{1,0:T(8,128)} %fusion.56, bf16[1024,1536]{1,0:T(8,128)(2,1)} %all-gather.5.cloned.1.call-done, bf16[1536,384]{1,0:T(8,128)(2,1)S(1)} %copy-done), kind=kOutput, calls=%fused_computation.54 | convolution fusion | flops 1215823872 | bytes 8257536 | tf_op jit(solution)/shard_map/dot_general | solution.py:136
  114.3 0.9 copy-done.16
  115.1 1.4 fusion.35
  116.6 0.7 copy.38
  117.8 4.8 convolution_convert_fusion.2
  122.7 2.7 reshape.102
  125.4 9.5 %pad_maximum_fusion.2 = bf16[1179648]{0:T(1024)(128)(2,1)} fusion(bf16[589824]{0:T(1024)(128)(2,1)S(1)} %reshape.102, bf16[589824]{0:T(1024)(128)(2,1)S(1)} %reshape.101), kind=kLoop, calls=%fused_computation.43 | loop fusion | flops 4718592 | bytes 4718592 | tf_op jit(solution)/shard_map/concatenate | solution.py:51
  134.9 4.6 convolution_convert_fusion
  139.6 5.1 convert_element_type.119
  144.7 3.5 convolution_convert_fusion.1
  148.2 5.0 convert_element_type.109
  153.3 8.6 %all-gather.7.cloned.1.call-done = bf16[8,16,2,5,1536]{4,1,3,0,2:T(8,128)(2,1)} async-done(((bf16[1,16,2,5,1536]{4,1,3,0,2:T(8,128)(2,1)}), bf16[8,16,2,5,1536]{4,1,3,0,2:T(8,128)(2,1)}) %all-gather.7.cloned.1.call-update) | async-done | bytes 3932176 | tf_op jit(solution)/shard_map/all_gather | solution.py:106
  161.8 9.1 %fusion.24 = (bf16[8,16,2,5,768]{4,1,3,0,2:T(8,128)(2,1)S(1)}, f32[2,8,16,5,768]{4,2,3,1,0:T(8,128)}) fusion(bf16[8,16,2,5,1536]{4,1,3,0,2:T(8,128)(2,1)} %all-gather.7.cloned.1.call-done, bf16[2,1536,768]{2,1,0:T(8,128)(2,1)} %param.16), kind=kOutput, calls=%fused_computation.33 | convolution fusion | flops 3028746240 | bytes 14548992 | tf_op jit(solution)/shard_map/abjcd,jdf->abjcf/dot_general | solution.py:128
  171.0 1.3 copy-done.18
  172.2 6.2 %fusion.30 = bf16[8,16,2,5,1536]{4,1,3,0,2:T(8,128)(2,1)S(1)} fusion(bf16[8,16,2,5,768]{4,1,3,0,2:T(8,128)(2,1)S(1)} %get-tuple-element.11, bf16[2,768,1536]{2,1,0:T(8,128)(2,1)} %param.17), kind=kOutput, calls=%fused_computation.39 | convolution fusion | flops 3021864960 | bytes 10616832 | tf_op jit(solution)/shard_map/abjcf,jfd->abjcd/dot_general | solution.py:133
  178.4 5.2 copy.25
  183.7 10.9 %reshape_reshape.8 = bf16[8,245760]{1,0:T(8,128)(2,1)} reshape(bf16[8,16,2,5,1536]{4,3,2,1,0:T(8,128)(2,1)} %copy.25) | data formatting | bytes 7864320 | tf_op jit(solution)/shard_map/reshape;reshape | solution.py:39
  194.5 8.5 %pad_maximum_fusion = bf16[8,442368]{1,0:T(8,128)(2,1)} fusion(bf16[8,245760]{1,0:T(8,128)(2,1)} %reshape_reshape.8, bf16[8,196608]{1,0:T(8,128)(2,1)} %convert_element_type.109), kind=kLoop, calls=%fused_computation.6 | loop fusion | flops 14155776 | bytes 14155776 | tf_op jit(solution)/shard_map/concatenate | solution.py:39
  203.0 9.2 %reshape.95 = bf16[27648,128]{1,0:T(8,128)(2,1)} reshape(bf16[8,442368]{1,0:T(8,128)(2,1)} %pad_maximum_fusion) | data formatting | bytes 14155776 | tf_op jit(solution)/shard_map/reshape | solution.py:41
  212.5 9.9 %fusion.20 = bf16[8,16,2,5,768]{4,1,3,0,2:T(8,128)(2,1)S(1)} fusion(f32[2,8,16,5,768]{4,2,3,1,0:T(8,128)} %get-tuple-element.12, bf16[8,16,2,5,1536]{4,1,3,0,2:T(8,128)(2,1)} %all-gather.11.cloned.1.call-done, bf16[2,768,1536]{2,1,0:T(8,128)(2,1)} %param.17), kind=kOutput, calls=%fused_computation.26 | convolution fusion | flops 3039559680 | bytes 14548992 | tf_op jit(solution)/shard_map/abjcd,jfd->abjcf/dot_general | solution.py:147
  222.4 3.7 fusion.27
  226.2 5.3 copy.31
  231.5 10.8 %reshape_reshape.9 = bf16[8,245760]{1,0:T(8,128)(2,1)} reshape(bf16[8,16,2,5,1536]{4,3,2,1,0:T(8,128)(2,1)} %copy.31) | data formatting | bytes 7864320 | tf_op jit(solution)/shard_map/reshape;reshape | solution.py:39
  242.3 8.6 %pad_maximum_fusion.1 = bf16[8,442368]{1,0:T(8,128)(2,1)} fusion(bf16[8,245760]{1,0:T(8,128)(2,1)} %reshape_reshape.9, bf16[8,196608]{1,0:T(8,128)(2,1)} %convert_element_type.119), kind=kLoop, calls=%fused_computation.7 | loop fusion | flops 14155776 | bytes 14155776 | tf_op jit(solution)/shard_map/concatenate | solution.py:39
  250.9 9.1 %reshape.98 = bf16[27648,128]{1,0:T(8,128)(2,1)} reshape(bf16[8,442368]{1,0:T(8,128)(2,1)} %pad_maximum_fusion.1) | data formatting | bytes 14155776 | tf_op jit(solution)/shard_map/reshape | solution.py:41
  260.1 1.5 copy-done.19
  261.6 7.8 %bitcast_convert_fusion = bf16[2,768,1536]{2,1,0:T(8,128)(2,1)} fusion(bf16[8,16,2,5,1536]{4,1,3,0,2:T(8,128)(2,1)} %all-gather.11.cloned.1.call-done, bf16[8,16,2,5,768]{4,1,3,0,2:T(8,128)(2,1)S(1)} %copy-done.19), kind=kOutput, calls=%fused_computation.4 | convolution fusion | flops 3022258176 | bytes 10616832 | tf_op jit(solution)/shard_map/abjcf,abjcd->jfd/dot_general | solution.py:151
  269.4 5.6 bitcast_convert_fusion.1
  275.0 85.9 %all-reduce.4.cloned.1.call-done = bf16[1179648]{0:T(1024)(128)(2,1)} async-done(((bf16[1179648]{0:T(1024)(128)(2,1)}), bf16[1179648]{0:T(1024)(128)(2,1)}) %all-reduce.4.cloned.1.call-update) | async-done | bytes 2359312 | tf_op jit(solution)/shard_map/psum | solution.py:52
  360.9 1.8 fusion.55
  362.7 2.2 slice.57
  364.9 1.4 slice.55
  366.2 78.5 %reduce-scatter.3.cloned.1.call-done = bf16[3456,128]{1,0:T(8,128)(2,1)} async-done(((bf16[27648,128]{1,0:T(8,128)(2,1)}), bf16[3456,128]{1,0:T(8,128)(2,1)}) %reduce-scatter.3.cloned.1.call-update) | async-done | bytes 884752 | tf_op jit(solution)/shard_map/reduce_scatter | solution.py:42
  444.7 1.1 slice_convert_fusion.1
  446.5 1.2 copy.26
  447.7 7.7 %all-to-all-start.2 = ((bf16[16,2,5,1536]{3,1,2,0:T(2,128)(2,1)}), bf16[16,2,5,1536]{3,1,2,0:T(2,128)(2,1)S(1)}, u32[]{:S(2)}, u32[]{:S(2)}) async-start(bf16[16,2,5,1536]{3,1,2,0:T(2,128)(2,1)} %copy.26), calls=%async_computation.3 | async-start | bytes 983040 | tf_op jit(solution)/shard_map/all_to_all | solution.py:121
  455.4 74.2 %reduce-scatter.5.cloned.1.call-done = bf16[3456,128]{1,0:T(8,128)(2,1)} async-done(((bf16[27648,128]{1,0:T(8,128)(2,1)}), bf16[3456,128]{1,0:T(8,128)(2,1)}) %reduce-scatter.5.cloned.1.call-update) | async-done | bytes 884752 | tf_op jit(solution)/shard_map/reduce_scatter | solution.py:42
  529.6 1.0 slice_convert_fusion
  530.8 1.8 slice.67
  532.6 1.6 reshape.99
  534.2 1.2 copy.32
  535.4 0.8 copy-done.4
  536.2 7.9 %all-to-all-start.5 = ((bf16[16,2,5,1536]{3,1,2,0:T(2,128)(2,1)}), bf16[16,2,5,1536]{3,1,2,0:T(2,128)(2,1)}, u32[]{:S(2)}, u32[]{:S(2)}) async-start(bf16[16,2,5,1536]{3,1,2,0:T(2,128)(2,1)} %copy.32), calls=%async_computation.7 | async-start | bytes 983040 | tf_op jit(solution)/shard_map/all_to_all | solution.py:121
  544.1 1.1 copy.27
  545.2 1.0 reshape.97
  546.2 1.1 concatenate.16
  547.3 1.0 gather_fusion
  548.3 1.0 fusion.48
  549.8 5.2 all-to-all-done.5
  555.0 1.1 copy.33
  556.4 1.2 gather_fusion.1
  557.5 0.8 add_convert_fusion
  (81 shorter events, 7.8 us)
Async XLA Ops:
  7.2 100.9 %copy-start = (bf16[1536,384]{1,0:T(8,128)(2,1)S(1)}, bf16[1536,384]{1,0:T(8,128)(2,1)}, u32[]{:S(2)}) copy-start(bf16[1536,384]{1,0:T(8,128)(2,1)} %param.18) | copy-start | bytes 3538948
  7.2 62.9 %all-gather.9.cloned.1.call-start = ((), (), s32[]{:S(2)}) async-start(), calls=%async_computation.11 | async-start | bytes 3538944 | tf_op jit(solution)/shard_map/all_gather | solution.py:105
  7.9 100.2 %all-gather.5.cloned.1.call-start = ((), (), s32[]{:S(2)}) async-start(), calls=%async_computation.8 | async-start | bytes 3538944 | tf_op jit(solution)/shard_map/all_gather | solution.py:105
  8.7 153.2 %all-gather.7.cloned.1.call-start = ((), (), s32[]{:S(2)}) async-start(), calls=%async_computation.9 | async-start | bytes 4423680 | tf_op jit(solution)/shard_map/all_gather | solution.py:106
  11.5 28.6 %copy-start.7 = (s32[128]{0:T(128)S(1)}, s32[128]{0:T(128)}, u32[]{:S(2)}) copy-start(s32[128]{0:T(128)} %param.13) | copy-start | bytes 1540
  11.5 28.6 %copy-start.9 = (s32[128]{0:T(128)S(1)}, s32[128]{0:T(128)}, u32[]{:S(2)}) copy-start(s32[128]{0:T(128)} %param.14) | copy-start | bytes 1540
  11.5 28.6 %copy-start.11 = (f32[128]{0:T(128)S(1)}, f32[128]{0:T(128)}, u32[]{:S(2)}) copy-start(f32[128]{0:T(128)} %param.11) | copy-start | bytes 1540
  11.5 29.2 %copy-start.2 = (bf16[128,1536]{1,0:T(8,128)(2,1)S(1)}, bf16[128,1536]{1,0:T(8,128)(2,1)}, u32[]{:S(2)}) copy-start(bf16[128,1536]{1,0:T(8,128)(2,1)} %param.15) | copy-start | bytes 1179652
  40.1 0.5 copy-start.5
  42.7 27.4 %copy-start.14 = (bf16[384,1536]{1,0:T(8,128)(2,1)S(1)}, bf16[384,1536]{1,0:T(8,128)(2,1)}, u32[]{:S(2)}) copy-start(bf16[384,1536]{1,0:T(8,128)(2,1)} %param.19) | copy-start | bytes 3538948
  50.2 18.7 %all-to-all-start.4 = ((bf16[8,2,1,2,5,1536]{5,3,4,2,1,0:T(2,128)(2,1)}), bf16[8,2,1,2,5,1536]{5,3,4,2,1,0:T(2,128)(2,1)S(1)}, u32[]{:S(2)}, u32[]{:S(2)}) async-start(bf16[8,2,1,2,5,1536]{5,3,4,2,1,0:T(2,128)(2,1)} %copy.29), calls=%async_computation.5 | async-start | bytes 983040 | tf_op jit(solution)/shard_map/all_to_all | solution.py:26
  53.7 158.8 %all-gather.11.cloned.1.call-start = ((), (), s32[]{:S(2)}) async-start(), calls=%async_computation.12 | async-start | bytes 4423680 | tf_op jit(solution)/shard_map/all_gather | solution.py:106
  69.8 291.1 %all-reduce.4.cloned.1.call-start = ((), (), s32[]{:S(2)}) async-start(), calls=%async_computation.14 | async-start | bytes 4718592 | tf_op jit(solution)/shard_map/psum | solution.py:52
  108.1 7.0 %copy-start.13 = (bf16[1024,1536]{1,0:T(8,128)(2,1)S(1)}, bf16[1024,1536]{1,0:T(8,128)(2,1)}, u32[]{:S(2)}) copy-start(bf16[1024,1536]{1,0:T(8,128)(2,1)} %all-gather.5.cloned.1.call-done) | copy-start | bytes 9437188
  114.3 0.9 copy-start.16
  139.6 5.1 copy-start.15
  139.6 5.1 copy-start.17
  153.2 291.5 %reduce-scatter.3.cloned.1.call-start = ((), (), s32[]{:S(2)}) async-start(), calls=%async_computation.10 | async-start | bytes 7962624 | tf_op jit(solution)/shard_map/reduce_scatter | solution.py:42
  171.0 1.3 copy-start.18
  203.0 19.4 %slice-start.1 = ((s8[4718592]{0:T(1024)(128)(4,1)}), s8[524288]{0:T(1024)(128)(4,1)S(1)}, s32[]{:S(2)}) async-start(s8[4718592]{0:T(1024)(128)(4,1)} %bitcast.86), calls=%async_computation.16 | async-start | bytes 1048576
  212.5 9.9 %slice-start.2 = ((s8[4718592]{0:T(1024)(128)(4,1)}), s8[4194304]{0:T(1024)(128)(4,1)S(1)}, s32[]{:S(2)}) async-start(s8[4718592]{0:T(1024)(128)(4,1)} %bitcast.86), calls=%async_computation.17 | async-start | bytes 8388608
  222.4 3.7 copy-start.20
  242.3 287.3 %reduce-scatter.5.cloned.1.call-start = ((), (), s32[]{:S(2)}) async-start(), calls=%async_computation.13 | async-start | bytes 7962624 | tf_op jit(solution)/shard_map/reduce_scatter | solution.py:42
  260.1 1.6 copy-start.19
  261.6 7.8 %copy-start.12 = (bf16[8,16,2,5,1536]{4,1,3,0,2:T(8,128)(2,1)S(1)}, bf16[8,16,2,5,1536]{4,1,3,0,2:T(8,128)(2,1)}, u32[]{:S(2)}) copy-start(bf16[8,16,2,5,1536]{4,1,3,0,2:T(8,128)(2,1)} %all-gather.7.cloned.1.call-done) | copy-start | bytes 11796484
  261.6 7.8 %copy-start.21 = (bf16[8,16,2,5,768]{4,1,3,0,2:T(8,128)(2,1)S(1)}, bf16[8,16,2,5,768]{4,1,3,0,2:T(8,128)(2,1)}, u32[]{:S(2)}) copy-start(bf16[8,16,2,5,768]{4,1,3,0,2:T(8,128)(2,1)} %copy-done.20) | copy-start | bytes 5898244
  444.7 1.2 slice-start
  447.7 87.7 %all-to-all-start.2 = ((bf16[16,2,5,1536]{3,1,2,0:T(2,128)(2,1)}), bf16[16,2,5,1536]{3,1,2,0:T(2,128)(2,1)S(1)}, u32[]{:S(2)}, u32[]{:S(2)}) async-start(bf16[16,2,5,1536]{3,1,2,0:T(2,128)(2,1)} %copy.26), calls=%async_computation.3 | async-start | bytes 983040 | tf_op jit(solution)/shard_map/all_to_all | solution.py:121
  535.4 0.8 copy-start.4
  536.2 18.8 %all-to-all-start.5 = ((bf16[16,2,5,1536]{3,1,2,0:T(2,128)(2,1)}), bf16[16,2,5,1536]{3,1,2,0:T(2,128)(2,1)}, u32[]{:S(2)}, u32[]{:S(2)}) async-start(bf16[16,2,5,1536]{3,1,2,0:T(2,128)(2,1)} %copy.32), calls=%async_computation.7 | async-start | bytes 983040 | tf_op jit(solution)/shard_map/all_to_all | solution.py:121
  545.2 3.1 copy-start.3
  545.2 3.1 copy-start.6
  546.2 3.1 copy-start.8
  546.2 3.1 copy-start.10
  556.1 2.2 copy-start.1
Sparse Core Ops, SparseCore 0:
  9.6 50.7 all-gather.8
  62.1 45.9 all-gather.4
  109.8 52.0 all-gather.6
  163.3 49.1 all-gather.10
  214.8 146.0 all-reduce.3
  363.2 81.4 reduce-scatter.2
  447.1 82.4 reduce-scatter.4
where the time goes:
time: 571 us; the launch traced here: 566 us
  waiting for transfers between devices  302 us (53%)
  local copies, waits for them, and re-layouts  94.5 us (17%)
  matrix products  67.7 us (12%)
  other arithmetic  33.7 us (6%)
  blocking collectives  33.4 us (6%)
  starting transfers between devices  19.5 us (3%)
  between operations  15.1 us (3%)
    reduce_scatter x2, waiting for transfers between devices, sum_packed(): lax.psum_scatter(lines, axis, tiled=True).reshape(-1)  153 us
    psum x1, waiting for transfers between devices, in_one(): running = lax.psum(flat, axis)  85.9 us
    all_to_all x3, blocking collectives, exchange_in_order(): whole = lax.all_to_all(whole, axes[k], k, k, tiled=True)  33.4 us
    all_gather x2, waiting for transfers between devices, to_column(): lax.all_gather(row_values, 'dp', axis=0, tiled=True)  33.2 us
    another operation x2, local copies, waits for them, and re-layouts, sum_packed(): lines = jnp.concatenate([b.reshape(peers, -1) for b in blocks], axis=1)  21.7 us
    reshape x2, local copies, waits for them, and re-layouts, sum_packed(): jnp.pad(lines, ((0, 0), (0, rows * 128 - lines.shape[1]))).reshape(-1, 128)  18.3 us
    concatenate x2, other arithmetic, sum_packed(): lines = jnp.concatenate([b.reshape(peers, -1) for b in blocks], axis=1)  17 us
    all_to_all x2, starting transfers between devices, from_column(): lax.all_to_all(expert_sum[0].astype(jnp.bfloat16), EXPERT, split_axis=0,...  15.5 us
  transfers between devices with their start and end apart: 10, of which 8 were waited for; matrix products, arithmetic and copies ran while one was open for 33% of the time, Pallas kernels for 0%

commit v1 on v0

--- a/solution.py
+++ b/solution.py
@@ -102,7 +102,9 @@
         )
         arrived = exchange_by_chip(own_buffer, (("expert_0", "expert_1"), "expert_2"), (1, 0), 0, 0)
         col_rows, column = (
-            lax.all_gather(row_values, "dp", axis=0, tiled=True),
+            jnp.concatenate(
+                lax.all_to_all(jnp.stack([row_values] * lax.axis_size("dp")), "dp", 0, 0), axis=0
+            ),
             lax.all_gather(arrived[None], "dp", axis=0, tiled=True),
         )
         return (col_rows, column)

time: 571 us -> 531 us (0.930)
  waiting for transfers between devices: 302 us -> 183 us
  blocking collectives: 33.4 us -> 107 us
    reduce_scatter x2, waiting for transfers between devices: 153 us -> 24.1 us  [sum_packed(): lax.psum_scatter(lines, axis, tiled=True).reshape(-1)]
    all_to_all x0 -> x1, blocking collectives: none -> 59.4 us  [to_column(): lax.all_to_all(jnp.stack([row_values] * lax.axis_size('dp')), 'dp', 0, 0)]
    all_gather x2 -> x0, waiting for transfers between devices: 33.2 us -> none  [to_column(): lax.all_gather(row_values, 'dp', axis=0, tiled=True)]
    all_to_all x1, waiting for transfers between devices: 14.5 us -> 44.6 us  [to_column(): lax.all_to_all(jnp.stack([row_values] * lax.axis_size('dp')), 'dp', 0, 0)]
    psum x1, waiting for transfers between devices: 85.9 us -> 109 us  [in_one(): running = lax.psum(flat, axis)]
    all_to_all x3 -> x4, blocking collectives: 33.4 us -> 47.8 us  [exchange_in_order(): whole = lax.all_to_all(whole, axes[k], k, k, tiled=True)]
    all_gather x2, waiting for transfers between devices: 8.86 us -> 0.02 us  [to_column(): lax.all_gather(arrived[None], 'dp', axis=0, tiled=True)]
  transfers between devices with their start and end apart: 10 -> 8, of which waited for: 8 -> 4; matrix products, arithmetic and copies ran while one was open for 33% -> 35% of each run, Pallas kernels for 0% -> 0%
where the time goes in v1:
time: 531 us; the launch traced here: 522 us
  waiting for transfers between devices  183 us (34%)
  blocking collectives  107 us (20%)
  local copies, waits for them, and re-layouts  93.2 us (18%)
  matrix products  65.9 us (12%)
  other arithmetic  33.7 us (6%)
  starting transfers between devices  22.7 us (4%)
  between operations  16.2 us (3%)
    psum x1, waiting for transfers between devices, in_one(): running = lax.psum(flat, axis)  109 us
    all_to_all x1, blocking collectives, to_column(): lax.all_to_all(jnp.stack([row_values] * lax.axis_size('dp')), 'dp', 0, 0)  59.4 us
    all_to_all x4, blocking collectives, exchange_in_order(): whole = lax.all_to_all(whole, axes[k], k, k, tiled=True)  47.8 us
    all_to_all x1, waiting for transfers between devices, to_column(): lax.all_to_all(jnp.stack([row_values] * lax.axis_size('dp')), 'dp', 0, 0)  44.6 us
    reduce_scatter x2, waiting for transfers between devices, sum_packed(): lax.psum_scatter(lines, axis, tiled=True).reshape(-1)  24.1 us
    another operation x2, local copies, waits for them, and re-layouts, sum_packed(): lines = jnp.concatenate([b.reshape(peers, -1) for b in blocks], axis=1)  21.6 us
    reshape x2, local copies, waits for them, and re-layouts, sum_packed(): jnp.pad(lines, ((0, 0), (0, rows * 128 - lines.shape[1]))).reshape(-1, 128)  18.4 us
    all_to_all x2, starting transfers between devices, from_column(): lax.all_to_all(expert_sum[0].astype(jnp.bfloat16), EXPERT, split_axis=0,...  17.8 us
  transfers between devices with their start and end apart: 8, of which 4 were waited for; matrix products, arithmetic and copies ran while one was open for 35% of the time, Pallas kernels for 0%

profile of v1, /device:TPU:1, one launch (start us, length us, event | category | flops | bytes accessed | tf_op | source)
XLA Modules:
  0.0 522.2 jit_solution(16390946013694561932)
XLA Ops:
  8.1 0.8 compare_select_fusion
  8.8 1.8 scatter_custom_fusion
  11.3 5.1 all_to_all.40
  16.8 17.9 %all_to_all.41 = bf16[8,2,1,2,5,1536]{5,3,4,2,1,0:T(2,128)(2,1)S(1)} all-to-all(bf16[8,2,1,2,5,1536]{5,3,4,2,1,0:T(2,128)(2,1)S(1)} %copy.23), channel_id=1, replica_groups=mesh['dp'=8,'expert_0'=4,'expert_1'=2,'expert_2'=2] {'expert_0','expert_1'}, dimensions={0} | all-to-all | bytes 983040 | tf_op jit(solution)/shard_map/all_to_all | solution.py:26
  34.6 0.8 copy.43
  35.6 1.4 scatter_custom_fusion.1
  37.6 5.5 %all_to_all.42 = bf16[8,2,1,2,5,1536]{5,0,4,3,2,1:T(8,128)(2,1)S(1)} all-to-all(bf16[8,2,1,2,5,1536]{5,0,4,3,2,1:T(8,128)(2,1)S(1)} %copy.28), channel_id=1, replica_groups=mesh['dp'=8,'expert_0'=4,'expert_1'=2,'expert_2'=2] {'expert_2'}, dimensions={1} | all-to-all | bytes 983040 | tf_op jit(solution)/shard_map/all_to_all | solution.py:26
  43.4 19.3 %all_to_all.43 = bf16[8,2,1,2,5,1536]{5,3,4,2,1,0:T(2,128)(2,1)S(1)} all-to-all(bf16[8,2,1,2,5,1536]{5,3,4,2,1,0:T(2,128)(2,1)S(1)} %copy.29), channel_id=1, replica_groups=mesh['dp'=8,'expert_0'=4,'expert_1'=2,'expert_2'=2] {'expert_0','expert_1'}, dimensions={0} | all-to-all | bytes 983040 | tf_op jit(solution)/shard_map/all_to_all | solution.py:26
  63.0 59.4 %all_to_all.44 = bf16[8,128,1536]{2,1,0:T(8,128)(2,1)} all-to-all(bf16[8,128,1536]{2,1,0:T(8,128)(2,1)S(1)} %stack.5), channel_id=1, replica_groups=mesh['dp'=8,'expert_0'=4,'expert_1'=2,'expert_2'=2] {'dp'}, dimensions={0} | all-to-all | bytes 6291456 | tf_op jit(solution)/shard_map/all_to_all | solution.py:106
  122.4 1.9 stack.4
  124.4 4.4 all-to-all-start
  128.9 0.6 pad_clamp_fusion
  129.5 0.9 copy.44
  130.4 4.0 fusion.56
  134.4 44.6 %all-to-all-done = bf16[8,128,1536]{2,1,0:T(8,128)(2,1)} async-done(((bf16[8,128,1536]{2,1,0:T(8,128)(2,1)}), bf16[8,128,1536]{2,1,0:T(8,128)(2,1)}, u32[]{:S(2)}, u32[]{:S(2)}) %all-to-all-start) | async-done | bytes 3145760 | tf_op jit(solution)/shard_map/all_to_all | solution.py:106
  179.1 4.7 fusion.44
  183.8 2.5 convolution_convert_fusion.2
  186.2 3.3 fusion.35
  189.6 0.9 copy.38
  191.0 2.8 reshape.114
  193.8 9.3 %pad_maximum_fusion.2 = bf16[1179648]{0:T(1024)(128)(2,1)} fusion(bf16[589824]{0:T(1024)(128)(2,1)S(1)} %reshape.114, bf16[589824]{0:T(1024)(128)(2,1)S(1)} %reshape.113), kind=kLoop, calls=%fused_computation.43 | loop fusion | flops 4718592 | bytes 4718592 | tf_op jit(solution)/shard_map/concatenate | solution.py:51
  203.0 4.6 convolution_convert_fusion
  207.7 5.1 convert_element_type.119
  212.8 3.5 convolution_convert_fusion.1
  216.3 4.9 convert_element_type.109
  221.6 9.1 %fusion.24 = (bf16[8,16,2,5,768]{4,1,3,0,2:T(8,128)(2,1)S(1)}, f32[2,8,16,5,768]{4,2,3,1,0:T(8,128)}) fusion(bf16[8,16,2,5,1536]{4,1,3,0,2:T(8,128)(2,1)} %all-gather.3.cloned.1.call-done, bf16[2,1536,768]{2,1,0:T(8,128)(2,1)} %param.16), kind=kOutput, calls=%fused_computation.33 | convolution fusion | flops 3028746240 | bytes 14548992 | tf_op jit(solution)/shard_map/abjcd,jdf->abjcf/dot_general | solution.py:130
  230.7 1.3 copy-done.19
  231.9 5.7 %fusion.30 = bf16[8,16,2,5,1536]{4,1,3,0,2:T(8,128)(2,1)S(1)} fusion(bf16[8,16,2,5,768]{4,1,3,0,2:T(8,128)(2,1)S(1)} %get-tuple-element.11, bf16[2,768,1536]{2,1,0:T(8,128)(2,1)} %param.17), kind=kOutput, calls=%fused_computation.39 | convolution fusion | flops 3021864960 | bytes 10616832 | tf_op jit(solution)/shard_map/abjcf,jfd->abjcd/dot_general | solution.py:135
  237.7 5.2 copy.25
  242.9 10.8 %reshape_reshape.8 = bf16[8,245760]{1,0:T(8,128)(2,1)} reshape(bf16[8,16,2,5,1536]{4,3,2,1,0:T(8,128)(2,1)} %copy.25) | data formatting | bytes 7864320 | tf_op jit(solution)/shard_map/reshape;reshape | solution.py:39
  253.7 8.7 %pad_maximum_fusion = bf16[8,442368]{1,0:T(8,128)(2,1)} fusion(bf16[8,245760]{1,0:T(8,128)(2,1)} %reshape_reshape.8, bf16[8,196608]{1,0:T(8,128)(2,1)} %convert_element_type.109), kind=kLoop, calls=%fused_computation.6 | loop fusion | flops 14155776 | bytes 14155776 | tf_op jit(solution)/shard_map/concatenate | solution.py:39
  262.4 9.2 %reshape.106 = bf16[27648,128]{1,0:T(8,128)(2,1)} reshape(bf16[8,442368]{1,0:T(8,128)(2,1)} %pad_maximum_fusion) | data formatting | bytes 14155776 | tf_op jit(solution)/shard_map/reshape | solution.py:41
  271.6 9.9 %fusion.20 = bf16[8,16,2,5,768]{4,1,3,0,2:T(8,128)(2,1)S(1)} fusion(f32[2,8,16,5,768]{4,2,3,1,0:T(8,128)} %get-tuple-element.12, bf16[8,16,2,5,1536]{4,1,3,0,2:T(8,128)(2,1)} %all-gather.5.cloned.1.call-done, bf16[2,768,1536]{2,1,0:T(8,128)(2,1)} %param.17), kind=kOutput, calls=%fused_computation.26 | convolution fusion | flops 3039559680 | bytes 14548992 | tf_op jit(solution)/shard_map/abjcd,jfd->abjcf/dot_general | solution.py:149
  281.5 3.7 fusion.27
  285.2 5.3 %copy.31 = bf16[8,16,2,5,1536]{4,3,2,1,0:T(8,128)(2,1)} copy(bf16[8,16,2,5,1536]{4,1,3,0,2:T(8,128)(2,1)S(1)} %fusion.27) | data formatting | bytes 7864320 | tf_op jit(solution)/shard_map/convert_element_type | solution.py:117
  290.5 10.8 %reshape_reshape.9 = bf16[8,245760]{1,0:T(8,128)(2,1)} reshape(bf16[8,16,2,5,1536]{4,3,2,1,0:T(8,128)(2,1)} %copy.31) | data formatting | bytes 7864320 | tf_op jit(solution)/shard_map/reshape;reshape | solution.py:39
  301.4 8.5 %pad_maximum_fusion.1 = bf16[8,442368]{1,0:T(8,128)(2,1)} fusion(bf16[8,245760]{1,0:T(8,128)(2,1)} %reshape_reshape.9, bf16[8,196608]{1,0:T(8,128)(2,1)} %convert_element_type.119), kind=kLoop, calls=%fused_computation.7 | loop fusion | flops 14155776 | bytes 14155776 | tf_op jit(solution)/shard_map/concatenate | solution.py:39
  309.9 9.2 %reshape.110 = bf16[27648,128]{1,0:T(8,128)(2,1)} reshape(bf16[8,442368]{1,0:T(8,128)(2,1)} %pad_maximum_fusion.1) | data formatting | bytes 14155776 | tf_op jit(solution)/shard_map/reshape | solution.py:41
  319.1 109.3 %all-reduce.4.cloned.1.call-done = bf16[1179648]{0:T(1024)(128)(2,1)} async-done(((bf16[1179648]{0:T(1024)(128)(2,1)}), bf16[1179648]{0:T(1024)(128)(2,1)}) %all-reduce.4.cloned.1.call-update) | async-done | bytes 2359312 | tf_op jit(solution)/shard_map/psum | solution.py:52
  428.5 1.8 fusion.55
  430.3 2.2 slice.57
  432.4 1.4 slice.55
  433.8 9.0 %bitcast_convert_fusion = bf16[2,768,1536]{2,1,0:T(8,128)(2,1)} fusion(bf16[8,16,2,5,1536]{4,1,3,0,2:T(8,128)(2,1)} %all-gather.5.cloned.1.call-done, bf16[8,16,2,5,768]{4,1,3,0,2:T(8,128)(2,1)} %copy-done.19), kind=kOutput, calls=%fused_computation.4 | convolution fusion | flops 3022258176 | bytes 10616832 | tf_op jit(solution)/shard_map/abjcf,abjcd->jfd/dot_general | solution.py:153
  442.8 5.8 %bitcast_convert_fusion.1 = bf16[2,1536,768]{2,1,0:T(8,128)(2,1)} fusion(bf16[8,16,2,5,1536]{4,1,3,0,2:T(8,128)(2,1)S(1)} %copy-done.14, bf16[8,16,2,5,768]{4,1,3,0,2:T(8,128)(2,1)S(1)} %copy-done.21), kind=kOutput, calls=%fused_computation.5 | convolution fusion | flops 3022258176 | bytes 10616832 | tf_op jit(solution)/shard_map/abjcd,abjcf->jdf/dot_general | solution.py:156
  448.7 1.1 slice_convert_fusion.1
  449.9 0.6 reshape.107
  450.5 1.2 copy.26
  451.7 10.7 %all-to-all-start.3 = ((bf16[16,2,5,1536]{3,1,2,0:T(2,128)(2,1)}), bf16[16,2,5,1536]{3,1,2,0:T(2,128)(2,1)S(1)}, u32[]{:S(2)}, u32[]{:S(2)}) async-start(bf16[16,2,5,1536]{3,1,2,0:T(2,128)(2,1)} %copy.26), calls=%async_computation.4 | async-start | bytes 983040 | tf_op jit(solution)/shard_map/all_to_all | solution.py:123
  462.4 24.1 %reduce-scatter.5.cloned.1.call-done = bf16[3456,128]{1,0:T(8,128)(2,1)} async-done(((bf16[27648,128]{1,0:T(8,128)(2,1)}), bf16[3456,128]{1,0:T(8,128)(2,1)}) %reduce-scatter.5.cloned.1.call-update) | async-done | bytes 884752 | tf_op jit(solution)/shard_map/reduce_scatter | solution.py:42
  486.5 1.0 slice_convert_fusion
  487.7 1.8 slice.67
  489.5 1.6 reshape.111
  491.1 1.2 copy.32
  492.3 0.8 copy-done.5
  493.1 7.1 %all-to-all-start.7 = ((bf16[16,2,5,1536]{3,1,2,0:T(2,128)(2,1)}), bf16[16,2,5,1536]{3,1,2,0:T(2,128)(2,1)}, u32[]{:S(2)}, u32[]{:S(2)}) async-start(bf16[16,2,5,1536]{3,1,2,0:T(2,128)(2,1)} %copy.32), calls=%async_computation.9 | async-start | bytes 983040 | tf_op jit(solution)/shard_map/all_to_all | solution.py:123
  500.2 1.1 copy.27
  501.4 1.0 reshape.108
  502.4 1.1 concatenate.16
  503.5 1.0 gather_fusion
  504.5 1.0 fusion.48
  506.0 5.2 %all-to-all-done.7 = bf16[16,2,5,1536]{3,1,2,0:T(2,128)(2,1)} async-done(((bf16[16,2,5,1536]{3,1,2,0:T(2,128)(2,1)}), bf16[16,2,5,1536]{3,1,2,0:T(2,128)(2,1)}, u32[]{:S(2)}, u32[]{:S(2)}) %all-to-all-start.7) | async-done | bytes 491552 | tf_op jit(solution)/shard_map/all_to_all | solution.py:123
  511.2 1.1 copy.33
  512.6 1.2 gather_fusion.1
  513.8 0.8 add_convert_fusion
  (79 shorter events, 4.4 us)
Async XLA Ops:
  8.0 171.1 %copy-start = (bf16[1536,384]{1,0:T(8,128)(2,1)S(1)}, bf16[1536,384]{1,0:T(8,128)(2,1)}, u32[]{:S(2)}) copy-start(bf16[1536,384]{1,0:T(8,128)(2,1)} %param.18) | copy-start | bytes 3538948
  8.0 213.5 %all-gather.3.cloned.1.call-start = ((), (), s32[]{:S(2)}) async-start(), calls=%async_computation.10 | async-start | bytes 4423680 | tf_op jit(solution)/shard_map/all_gather | solution.py:108
  10.9 24.6 %copy-start.9 = (s32[128]{0:T(128)S(1)}, s32[128]{0:T(128)}, u32[]{:S(2)}) copy-start(s32[128]{0:T(128)} %param.13) | copy-start | bytes 1540
  10.9 24.6 %copy-start.11 = (s32[128]{0:T(128)S(1)}, s32[128]{0:T(128)}, u32[]{:S(2)}) copy-start(s32[128]{0:T(128)} %param.14) | copy-start | bytes 1540
  10.9 24.6 %copy-start.13 = (f32[128]{0:T(128)S(1)}, f32[128]{0:T(128)}, u32[]{:S(2)}) copy-start(f32[128]{0:T(128)} %param.11) | copy-start | bytes 1540
  10.9 24.6 %copy-start.2 = (bf16[128,1536]{1,0:T(8,128)(2,1)S(1)}, bf16[128,1536]{1,0:T(8,128)(2,1)}, u32[]{:S(2)}) copy-start(bf16[128,1536]{1,0:T(8,128)(2,1)} %param.15) | copy-start | bytes 1179652
  35.6 1.4 copy-start.7
  63.0 59.4 %copy-start.6 = (bf16[128,1536]{1,0:T(8,128)(2,1)S(1)}, bf16[128,1536]{1,0:T(8,128)(2,1)}, u32[]{:S(2)}) copy-start(bf16[128,1536]{1,0:T(8,128)(2,1)} %param.10) | copy-start | bytes 1179652
  124.4 54.7 %all-to-all-start = ((bf16[8,128,1536]{2,1,0:T(8,128)(2,1)}), bf16[8,128,1536]{2,1,0:T(8,128)(2,1)}, u32[]{:S(2)}, u32[]{:S(2)}) async-start(bf16[8,128,1536]{2,1,0:T(8,128)(2,1)} %stack.4), calls=%async_computation | async-start | bytes 6291456 | tf_op jit(solution)/shard_map/all_to_all | solution.py:106
  128.8 142.7 %all-gather.5.cloned.1.call-start = ((), (), s32[]{:S(2)}) async-start(), calls=%async_computation.12 | async-start | bytes 4423680 | tf_op jit(solution)/shard_map/all_gather | solution.py:108
  130.4 298.1 %all-reduce.4.cloned.1.call-start = ((), (), s32[]{:S(2)}) async-start(), calls=%async_computation.14 | async-start | bytes 4718592 | tf_op jit(solution)/shard_map/psum | solution.py:52
  179.1 4.7 copy-start.4
  183.7 2.5 copy-start.17
  183.7 2.5 copy-start.16
  207.7 5.1 copy-start.15
  207.7 5.1 copy-start.18
  221.3 227.4 %reduce-scatter.3.cloned.1.call-start = ((), (), s32[]{:S(2)}) async-start(), calls=%async_computation.11 | async-start | bytes 7962624 | tf_op jit(solution)/shard_map/reduce_scatter | solution.py:42
  230.7 1.3 copy-start.19
  262.4 19.1 %slice-start.1 = ((s8[4718592]{0:T(1024)(128)(4,1)}), s8[524288]{0:T(1024)(128)(4,1)S(1)}, s32[]{:S(2)}) async-start(s8[4718592]{0:T(1024)(128)(4,1)} %bitcast.90), calls=%async_computation.16 | async-start | bytes 1048576
  271.6 9.9 %slice-start.2 = ((s8[4718592]{0:T(1024)(128)(4,1)}), s8[4194304]{0:T(1024)(128)(4,1)S(1)}, s32[]{:S(2)}) async-start(s8[4718592]{0:T(1024)(128)(4,1)} %bitcast.90), calls=%async_computation.17 | async-start | bytes 8388608
  281.5 3.7 copy-start.20
  301.3 185.1 %reduce-scatter.5.cloned.1.call-start = ((), (), s32[]{:S(2)}) async-start(), calls=%async_computation.13 | async-start | bytes 7962624 | tf_op jit(solution)/shard_map/reduce_scatter | solution.py:42
  433.8 9.0 %copy-start.14 = (bf16[8,16,2,5,1536]{4,1,3,0,2:T(8,128)(2,1)S(1)}, bf16[8,16,2,5,1536]{4,1,3,0,2:T(8,128)(2,1)}, u32[]{:S(2)}) copy-start(bf16[8,16,2,5,1536]{4,1,3,0,2:T(8,128)(2,1)} %all-gather.3.cloned.1.call-done) | copy-start | bytes 11796484
  433.8 9.0 %copy-start.21 = (bf16[8,16,2,5,768]{4,1,3,0,2:T(8,128)(2,1)S(1)}, bf16[8,16,2,5,768]{4,1,3,0,2:T(8,128)(2,1)}, u32[]{:S(2)}) copy-start(bf16[8,16,2,5,768]{4,1,3,0,2:T(8,128)(2,1)} %copy-done.20) | copy-start | bytes 5898244
  448.7 1.3 slice-start
  451.7 40.6 %all-to-all-start.3 = ((bf16[16,2,5,1536]{3,1,2,0:T(2,128)(2,1)}), bf16[16,2,5,1536]{3,1,2,0:T(2,128)(2,1)S(1)}, u32[]{:S(2)}, u32[]{:S(2)}) async-start(bf16[16,2,5,1536]{3,1,2,0:T(2,128)(2,1)} %copy.26), calls=%async_computation.4 | async-start | bytes 983040 | tf_op jit(solution)/shard_map/all_to_all | solution.py:123
  492.3 0.8 copy-start.5
  493.1 18.1 %all-to-all-start.7 = ((bf16[16,2,5,1536]{3,1,2,0:T(2,128)(2,1)}), bf16[16,2,5,1536]{3,1,2,0:T(2,128)(2,1)}, u32[]{:S(2)}, u32[]{:S(2)}) async-start(bf16[16,2,5,1536]{3,1,2,0:T(2,128)(2,1)} %copy.32), calls=%async_computation.9 | async-start | bytes 983040 | tf_op jit(solution)/shard_map/all_to_all | solution.py:123
  501.4 3.2 copy-start.3
  501.4 3.1 copy-start.8
  502.4 3.1 copy-start.10
  502.4 3.1 copy-start.12
  512.4 2.2 copy-start.1
Sparse Core Ops, SparseCore 0:
  35.6 82.5 all-gather.2
  131.3 74.7 all-gather.4
  301.5 95.7 reduce-scatter.2
  399.5 86.9 reduce-scatter.4
Sparse Core Ops, SparseCore 1:
  221.3 207.1 all-reduce.3
